TPU v7x, 256 devices: a whole 4x4x8 slice. The times are simulated.
256 devices in a mesh: pa: 32 (over z, x), sa: 8 (over y, core).
Axes of the slice: x: 4, y: 4, z: 8, core: 2. Of those that a mesh axis runs over, the one named last changes fastest.
Arguments:
- factors: bfloat16 [64, 16, 4096], P(None, None, 'pa'), may hold values from -6 to 6
- trade_weights: bfloat16 [64, 8192], P(None, 'pa'), may hold values from -0.75 to 0.75
- payoff_terms: bfloat16 [2, 8192], P(None, 'pa'), may hold values from -6 to 6
- set_blocks: int32 [32], replicated, may hold values from 1 to 4, 64 in all
- shock_pick: int32 [16], P('sa'), may hold values from 0 to 31
- shock_scale: float32 [32, 64], replicated, may hold values from 0.25 to 1.75
- shock_shift: float32 [32, 64], replicated, may hold values from -3 to 3
- discount: bfloat16 [16, 4096], P(None, 'pa'), may hold values from 0.5 to 1
- set_pd: float32 [32, 16], P('pa'), may hold values from 0.02 to 0.2
- own_pd: float32 [16], replicated, may hold values from 0.02 to 0.2
Outputs:
- exposure_profile: float32 [2, 32, 16, 16], P(None, 'pa', None, 'sa')
- set_xva: float32 [32, 16], P('pa', 'sa')
- total_xva: float32 [16], P('sa')
Inputs may be any that keep to these rules, and one draw needn't show every extreme that they name: `set_blocks`: each of the 32 netting sets holds whole consecutive blocks of 128 trades; the counts sum to 64.
All inputs are finite; a program needn't handle non-finite values.
Results may differ from a plain program's by a relative error of at most 0.00046.
Values may be sent and summed in bfloat16 or wider, within the bound.
A program may use at most 64 MiB of HBM per device.

v0:
```python
import math

import jax
import jax.numpy as jnp
from jax import lax
from jax.sharding import Mesh
from jax.sharding import PartitionSpec as P

TRADES = 8192
NSETS = 32
DATES = 16
PA = ("pa_0", "pa_1")


UNIT_SCALE = 0.0625


def whole_of(value, axes, dim):
    if not axes:
        return value
    nearer = lax.all_gather(value, axes[-1], axis=dim, tiled=True)
    return whole_of(nearer, axes[:-1], dim)


def from_everyone(value, axis):
    copies = jnp.broadcast_to(value, (lax.axis_size(axis), *value.shape))
    return lax.all_to_all(copies, axis, split_axis=0, concat_axis=0, tiled=True)


def of_everyone(value, axis):
    everything = from_everyone(value, axis)
    return jnp.sum(everything, axis=0)


def trade_members(set_blocks, block_count, set_count):
    set_ends = jnp.cumsum(set_blocks)
    block_ids = jnp.arange(block_count, dtype=jnp.int32)
    owners = jnp.sum((set_ends[None, :] <= block_ids[:, None]).astype(jnp.int32), axis=1)
    trade_owner = jnp.repeat(owners, 128)
    set_ids = jnp.arange(set_count, dtype=jnp.int32)
    return (trade_owner[None, :] == set_ids[:, None]).astype(jnp.bfloat16)


def net_trades(weights, trade_terms, members, shocked_rows):
    levels = lax.dot_general(
        weights, shocked_rows, (((0,), (0,)), ((), ())), preferred_element_type=jnp.float32
    )
    notional = trade_terms[0].astype(jnp.float32)[:, None]
    strike = trade_terms[1].astype(jnp.float32)[:, None]
    values = (notional * jax.nn.softplus(levels + strike)).astype(jnp.bfloat16)
    return jnp.dot(members, values, preferred_element_type=jnp.float32)


def on_device(
    factors,
    trade_weights,
    payoff_terms,
    set_blocks,
    shock_pick,
    shock_scale,
    shock_shift,
    discount,
    set_pd,
    own_pd,
):
    members = trade_members(set_blocks, TRADES // 128, NSETS)
    library = jnp.arange(shock_scale.shape[0], dtype=jnp.int32)
    pick_rows = (shock_pick[:, None] == library[None, :]).astype(jnp.float32)
    scale_rows = jnp.dot(pick_rows, shock_scale, precision=lax.Precision.HIGHEST).T
    shift_rows = jnp.dot(pick_rows, shock_shift, precision=lax.Precision.HIGHEST).T
    factor_count = factors.shape[0]
    shock_count = shock_pick.shape[0]
    path_total = factors.shape[2] * lax.axis_size(PA)
    shocked = (
        scale_rows[:, None, :, None] * factors.astype(jnp.float32)[:, :, None, :]
        + shift_rows[:, None, :, None]
    ).astype(jnp.bfloat16)
    row_block = shocked.reshape(factor_count, -1)
    empty = jnp.zeros((NSETS, row_block.shape[1]), jnp.float32)
    weights = whole_of(trade_weights, PA, 1)
    trade_terms = whole_of(payoff_terms, PA, 1)
    trade_count = weights.shape[1]
    block_width = math.gcd(trade_count, 1024)

    def add_block(position, inner):
        first_trade = position * block_width
        weights_part = lax.dynamic_slice_in_dim(weights, first_trade, block_width, 1)
        terms_part = lax.dynamic_slice_in_dim(trade_terms, first_trade, block_width, 1)
        members_part = lax.dynamic_slice_in_dim(members, first_trade, block_width, 1)
        return inner + net_trades(weights_part, terms_part, members_part, row_block)

    netted = UNIT_SCALE * lax.fori_loop(0, trade_count // block_width, add_block, empty)
    netted = netted.reshape(NSETS, DATES, shock_count, -1)
    exposure = netted * discount.astype(jnp.float32)[None, :, None, :]
    relaid = lax.all_to_all(exposure, PA, split_axis=0, concat_axis=3, tiled=True)
    positive = jnp.sum(jnp.maximum(relaid, 0.0), axis=3) / path_total
    negative = jnp.sum(jnp.minimum(relaid, 0.0), axis=3) / path_total
    profile = jnp.stack([positive, negative])
    adjustment = jnp.sum(set_pd[:, :, None] * profile[0], axis=1) + jnp.sum(
        own_pd[None, :, None] * profile[1], axis=1
    )
    shock_sums = of_everyone(jnp.sum(adjustment, axis=1), "sa")
    set_xva = adjustment - shock_sums[:, None] / (shock_count * lax.axis_size("sa"))
    total_xva = of_everyone(jnp.sum(adjustment, axis=0), PA)
    return (profile, set_xva, total_xva)


def solution(mesh):
    finer = Mesh(mesh.devices.reshape(8, 4, mesh.shape["sa"]), ("pa_0", "pa_1", "sa"))
    return jax.shard_map(
        on_device,
        mesh=finer,
        in_specs=(
            P(None, None, PA),
            P(None, PA),
            P(None, PA),
            P(),
            P("sa"),
            P(),
            P(),
            P(None, PA),
            P(PA, None),
            P(),
        ),
        out_specs=(P(None, PA, None, "sa"), P(PA, "sa"), P("sa")),
        check_vma=False,
    )
```

profile of v0, /device:TPU:1, one launch (start us, length us, event | category | flops | bytes accessed | tf_op | source)
XLA Modules:
  0.0 224.3 jit_solution(16464180763117609223)
XLA Ops:
  7.2 12.1 %all_gather.14 = bf16[64,1024]{1,0:T(8,128)(2,1)} all-gather(bf16[64,256]{1,0:T(8,128)(2,1)} %param.13), channel_id=1, replica_groups=mesh['pa_0'=8,'pa_1'=4,'sa'=8] {'pa_1'}, dimensions={1}, use_global_device_ids=true | all-gather | bytes 163840 | tf_op jit(solution)/shard_map/all_gather | solution.py:21
  19.3 0.7 copy.36
  20.4 0.8 convolution_bitcast_fusion.1
  21.3 0.9 convolution_bitcast_fusion
  22.2 1.0 convert_element_type.57
  23.4 6.9 %all_gather.12 = bf16[2,1024]{1,0:T(2,128)(2,1)S(1)} all-gather(bf16[2,256]{1,0:T(2,128)(2,1)S(1)} %copy-done.2), channel_id=1, replica_groups=mesh['pa_0'=8,'pa_1'=4,'sa'=8] {'pa_1'}, dimensions={1}, use_global_device_ids=true | all-gather | bytes 5120 | tf_op jit(solution)/shard_map/all_gather | solution.py:21
  30.2 22.5 %all_gather.13 = bf16[2,8192]{1,0:T(2,128)(2,1)S(1)} all-gather(bf16[2,1024]{1,0:T(2,128)(2,1)S(1)} %all_gather.12), channel_id=1, replica_groups=mesh['pa_0'=8,'pa_1'=4,'sa'=8] {'pa_0'}, dimensions={1}, use_global_device_ids=true | all-gather | bytes 36864 | tf_op jit(solution)/shard_map/all_gather | solution.py:21
  52.8 4.6 %all-gather.2.cloned.1.call-done = bf16[64,8192]{1,0:T(8,128)(2,1)} async-done(((bf16[64,1024]{1,0:T(8,128)(2,1)}), bf16[64,8192]{1,0:T(8,128)(2,1)}) %all-gather.2.cloned.1.call-update) | async-done | bytes 1048592 | tf_op jit(solution)/shard_map/all_gather | solution.py:21
  57.4 106.2 %while.14 = (s32[]{:T(128)}, f32[32,4096]{1,0:T(8,128)S(1)}, bf16[32,8192]{1,0:T(8,128)(2,1)S(1)}, bf16[2,8192]{1,0:T(2,128)(2,1)S(1)}, bf16[64,8192]{1,0:T(8,12...) while((s32[]{:T(128)}, f32[32,4096]{1,0:T(8,128)S(1)}, ...), condition=%wide.region_3.4_spmd.clone, body=%wide.region_2.3_spmd.clone.sunk | while | flops 844105728 | bytes 3889864 | solution.py:92
  58.4 12.2 %convolution_add_fusion.2 = f32[32,4096]{1,0:T(8,128)S(1)} fusion(bf16[64,4096]{1,0:T(8,128)(2,1)S(1)} %convert_element_type.89, f32[1024]{0:T(1024)S(1)} %bitcast.25, f32[1024]{0:T(1024)S(1)} %bitcast.24, f32[32,4096]{1,0:T(8,128)S(1)} %get-tuple-element.264, pred[]{:T(512)S(6)} %compare.3, bf16[64,8192]{1,0:T(8,128)(2,1)} %get-tuple-element.280, ...), kind=kOutput, calls=%fused_computation.4.clone.1 | convolution fusion | flops 843317248 | bytes 1779200 | tf_op jit(solution)/shard_map/while/body/eval_jaxpr/dot_general | solution.py:51
  70.7 0.6 add_convert_fusion.2
  71.7 12.2 %convolution_add_fusion.2 = f32[32,4096]{1,0:T(8,128)S(1)} fusion(bf16[64,4096]{1,0:T(8,128)(2,1)S(1)} %convert_element_type.89, f32[1024]{0:T(1024)S(1)} %bitcast.25, f32[1024]{0:T(1024)S(1)} %bitcast.24, f32[32,4096]{1,0:T(8,128)S(1)} %get-tuple-element.264, pred[]{:T(512)S(6)} %compare.3, bf16[64,8192]{1,0:T(8,128)(2,1)} %get-tuple-element.280, ...), kind=kOutput, calls=%fused_computation.4.clone.1 | convolution fusion | flops 843317248 | bytes 1779200 | tf_op jit(solution)/shard_map/while/body/eval_jaxpr/dot_general | solution.py:51
  84.0 0.6 add_convert_fusion.2
  84.9 12.2 %convolution_add_fusion.2 = f32[32,4096]{1,0:T(8,128)S(1)} fusion(bf16[64,4096]{1,0:T(8,128)(2,1)S(1)} %convert_element_type.89, f32[1024]{0:T(1024)S(1)} %bitcast.25, f32[1024]{0:T(1024)S(1)} %bitcast.24, f32[32,4096]{1,0:T(8,128)S(1)} %get-tuple-element.264, pred[]{:T(512)S(6)} %compare.3, bf16[64,8192]{1,0:T(8,128)(2,1)} %get-tuple-element.280, ...), kind=kOutput, calls=%fused_computation.4.clone.1 | convolution fusion | flops 843317248 | bytes 1779200 | tf_op jit(solution)/shard_map/while/body/eval_jaxpr/dot_general | solution.py:51
  98.2 12.2 %convolution_add_fusion.2 = f32[32,4096]{1,0:T(8,128)S(1)} fusion(bf16[64,4096]{1,0:T(8,128)(2,1)S(1)} %convert_element_type.89, f32[1024]{0:T(1024)S(1)} %bitcast.25, f32[1024]{0:T(1024)S(1)} %bitcast.24, f32[32,4096]{1,0:T(8,128)S(1)} %get-tuple-element.264, pred[]{:T(512)S(6)} %compare.3, bf16[64,8192]{1,0:T(8,128)(2,1)} %get-tuple-element.280, ...), kind=kOutput, calls=%fused_computation.4.clone.1 | convolution fusion | flops 843317248 | bytes 1779200 | tf_op jit(solution)/shard_map/while/body/eval_jaxpr/dot_general | solution.py:51
  111.4 12.2 %convolution_add_fusion.2 = f32[32,4096]{1,0:T(8,128)S(1)} fusion(bf16[64,4096]{1,0:T(8,128)(2,1)S(1)} %convert_element_type.89, f32[1024]{0:T(1024)S(1)} %bitcast.25, f32[1024]{0:T(1024)S(1)} %bitcast.24, f32[32,4096]{1,0:T(8,128)S(1)} %get-tuple-element.264, pred[]{:T(512)S(6)} %compare.3, bf16[64,8192]{1,0:T(8,128)(2,1)} %get-tuple-element.280, ...), kind=kOutput, calls=%fused_computation.4.clone.1 | convolution fusion | flops 843317248 | bytes 1779200 | tf_op jit(solution)/shard_map/while/body/eval_jaxpr/dot_general | solution.py:51
  124.7 12.2 %convolution_add_fusion.2 = f32[32,4096]{1,0:T(8,128)S(1)} fusion(bf16[64,4096]{1,0:T(8,128)(2,1)S(1)} %convert_element_type.89, f32[1024]{0:T(1024)S(1)} %bitcast.25, f32[1024]{0:T(1024)S(1)} %bitcast.24, f32[32,4096]{1,0:T(8,128)S(1)} %get-tuple-element.264, pred[]{:T(512)S(6)} %compare.3, bf16[64,8192]{1,0:T(8,128)(2,1)} %get-tuple-element.280, ...), kind=kOutput, calls=%fused_computation.4.clone.1 | convolution fusion | flops 843317248 | bytes 1779200 | tf_op jit(solution)/shard_map/while/body/eval_jaxpr/dot_general | solution.py:51
  137.9 12.2 %convolution_add_fusion.2 = f32[32,4096]{1,0:T(8,128)S(1)} fusion(bf16[64,4096]{1,0:T(8,128)(2,1)S(1)} %convert_element_type.89, f32[1024]{0:T(1024)S(1)} %bitcast.25, f32[1024]{0:T(1024)S(1)} %bitcast.24, f32[32,4096]{1,0:T(8,128)S(1)} %get-tuple-element.264, pred[]{:T(512)S(6)} %compare.3, bf16[64,8192]{1,0:T(8,128)(2,1)} %get-tuple-element.280, ...), kind=kOutput, calls=%fused_computation.4.clone.1 | convolution fusion | flops 843317248 | bytes 1779200 | tf_op jit(solution)/shard_map/while/body/eval_jaxpr/dot_general | solution.py:51
  151.2 12.2 %convolution_add_fusion.2 = f32[32,4096]{1,0:T(8,128)S(1)} fusion(bf16[64,4096]{1,0:T(8,128)(2,1)S(1)} %convert_element_type.89, f32[1024]{0:T(1024)S(1)} %bitcast.25, f32[1024]{0:T(1024)S(1)} %bitcast.24, f32[32,4096]{1,0:T(8,128)S(1)} %get-tuple-element.264, pred[]{:T(512)S(6)} %compare.3, bf16[64,8192]{1,0:T(8,128)(2,1)} %get-tuple-element.280, ...), kind=kOutput, calls=%fused_computation.4.clone.1 | convolution fusion | flops 843317248 | bytes 1779200 | tf_op jit(solution)/shard_map/while/body/eval_jaxpr/dot_general | solution.py:51
  164.1 1.0 broadcast_multiply_fusion
  165.1 7.1 %all-to-all-start = ((f32[32,16,2,128]{3,2,1,0:T(2,128)}), f32[32,16,2,128]{3,2,1,0:T(2,128)S(1)}, u32[]{:S(2)}, u32[]{:S(2)}) async-start(f32[32,16,2,128]{3,2,1,0:T(2,128)} %broadcast_multiply_fusion), calls=%async_computation | async-start | bytes 1048576 | tf_op jit(solution)/shard_map/all_to_all | solution.py:95
  172.3 12.8 %all-to-all-done = f32[32,16,2,128]{3,2,1,0:T(2,128)S(1)} async-done(((f32[32,16,2,128]{3,2,1,0:T(2,128)}), f32[32,16,2,128]{3,2,1,0:T(2,128)S(1)}, u32[]{:S(2)}, u32[]{:S(2)}) %all-to-all-start) | async-done | bytes 524320 | tf_op jit(solution)/shard_map/all_to_all | solution.py:95
  185.7 0.6 fusion.13
  186.3 1.2 broadcast_in_dim.16
  187.5 11.7 %all-to-all-start.1 = ((f32[8,1,1]{2,1,0:T(1,128)}), f32[8,1,1]{2,1,0:T(1,128)S(1)}, u32[]{:S(2)}, u32[]{:S(2)}) async-start(f32[8,1,1]{2,1,0:T(1,128)} %broadcast_in_dim.16), calls=%async_computation.1 | async-start | bytes 8192 | tf_op jit(solution)/shard_map/all_to_all | solution.py:27
  199.4 0.6 pad_maximum_fusion
  200.0 3.9 %all-to-all-done.1 = f32[8,1,1]{2,1,0:T(1,128)S(1)} async-done(((f32[8,1,1]{2,1,0:T(1,128)}), f32[8,1,1]{2,1,0:T(1,128)S(1)}, u32[]{:S(2)}, u32[]{:S(2)}) %all-to-all-start.1) | async-done | bytes 64 | tf_op jit(solution)/shard_map/all_to_all | solution.py:27
  203.8 0.6 broadcast_in_dim.17
  204.4 3.9 %all-to-all-start.2 = ((f32[32,1,2]{2,1,0:T(1,128)}), f32[32,1,2]{2,1,0:T(1,128)S(1)}, u32[]{:S(2)}, u32[]{:S(2)}) async-start(f32[32,1,2]{2,1,0:T(1,128)} %broadcast_in_dim.17), calls=%async_computation.2 | async-start | bytes 32768 | tf_op jit(solution)/shard_map/all_to_all | solution.py:27
  208.3 0.6 reduce_sum.82
  210.1 6.8 %all-to-all-done.2 = f32[32,1,2]{2,1,0:T(1,128)S(1)} async-done(((f32[32,1,2]{2,1,0:T(1,128)}), f32[32,1,2]{2,1,0:T(1,128)S(1)}, u32[]{:S(2)}, u32[]{:S(2)}) %all-to-all-start.2) | async-done | bytes 288 | tf_op jit(solution)/shard_map/all_to_all | solution.py:27
  216.9 0.6 reduce_sum.83
  (52 shorter events, 9.6 us)
Async XLA Ops:
  7.2 13.2 %copy-start = (f32[32,64]{1,0:T(8,128)S(1)}, f32[32,64]{1,0:T(8,128)}, u32[]{:S(2)}) copy-start(f32[32,64]{1,0:T(8,128)} %param.17) | copy-start | bytes 24580
  7.2 16.2 %copy-start.1 = (bf16[16,128]{1,0:T(8,128)(2,1)S(1)}, bf16[16,128]{1,0:T(8,128)(2,1)}, u32[]{:S(2)}) copy-start(bf16[16,128]{1,0:T(8,128)(2,1)} %param.19) | copy-start | bytes 12292
  7.2 16.2 %copy-start.2 = (bf16[2,256]{1,0:T(2,128)(2,1)S(1)}, bf16[2,256]{1,0:T(2,128)(2,1)}, u32[]{:S(2)}) copy-start(bf16[2,256]{1,0:T(2,128)(2,1)} %param.14) | copy-start | bytes 3076
  7.2 50.2 %all-gather.2.cloned.1.call-start = ((), (), s32[]{:S(2)}) async-start(), calls=%async_computation.3 | async-start | bytes 1179648 | tf_op jit(solution)/shard_map/all_gather | solution.py:21
  164.1 8.2 %copy-start.3 = (f32[16]{0:T(128)S(1)}, f32[16]{0:T(128)}, u32[]{:S(2)}) copy-start(f32[16]{0:T(128)} %param.21) | copy-start | bytes 196
  164.1 8.2 %copy-start.4 = (f32[1,16]{1,0:T(1,128)S(1)}, f32[1,16]{1,0:T(1,128)}, u32[]{:S(2)}) copy-start(f32[1,16]{1,0:T(1,128)} %param.20) | copy-start | bytes 196
  165.1 20.0 %all-to-all-start = ((f32[32,16,2,128]{3,2,1,0:T(2,128)}), f32[32,16,2,128]{3,2,1,0:T(2,128)S(1)}, u32[]{:S(2)}, u32[]{:S(2)}) async-start(f32[32,16,2,128]{3,2,1,0:T(2,128)} %broadcast_multiply_fusion), calls=%async_computation | async-start | bytes 1048576 | tf_op jit(solution)/shard_map/all_to_all | solution.py:95
  187.5 16.3 %all-to-all-start.1 = ((f32[8,1,1]{2,1,0:T(1,128)}), f32[8,1,1]{2,1,0:T(1,128)S(1)}, u32[]{:S(2)}, u32[]{:S(2)}) async-start(f32[8,1,1]{2,1,0:T(1,128)} %broadcast_in_dim.16), calls=%async_computation.1 | async-start | bytes 8192 | tf_op jit(solution)/shard_map/all_to_all | solution.py:27
  204.4 12.5 %all-to-all-start.2 = ((f32[32,1,2]{2,1,0:T(1,128)}), f32[32,1,2]{2,1,0:T(1,128)S(1)}, u32[]{:S(2)}, u32[]{:S(2)}) async-start(f32[32,1,2]{2,1,0:T(1,128)} %broadcast_in_dim.17), calls=%async_computation.2 | async-start | bytes 32768 | tf_op jit(solution)/shard_map/all_to_all | solution.py:27
Sparse Core Ops, SparseCore 0:
  19.4 37.8 all-gather.1
where the time goes:
time: 225 us; the launch traced here: 224 us
  matrix products  99.2 us (44%)
  blocking collectives  41.4 us (18%)
  waiting for transfers between devices  28 us (12%)
  starting transfers between devices  22.7 us (10%)
  between operations  14.8 us (7%)
  other arithmetic  11 us (5%)
  local copies, waits for them, and re-layouts  6.59 us (3%)
    dot_general x8, matrix products, net_trades(): return jnp.dot(members, values, preferred_element_type=jnp.float32)  97.4 us
    all_gather x3, blocking collectives, whole_of(): nearer = lax.all_gather(value, axes[-1], axis=dim, tiled=True)  41.4 us
    all_to_all x2, starting transfers between devices, from_everyone(): return lax.all_to_all(copies, axis, split_axis=0, concat_axis=0, tiled=True)  15.6 us
    all_to_all x1, waiting for transfers between devices, on_device(): lax.all_to_all(exposure, PA, split_axis=0, concat_axis=3, tiled=True)  12.8 us
    all_to_all x2, waiting for transfers between devices, from_everyone(): return lax.all_to_all(copies, axis, split_axis=0, concat_axis=0, tiled=True)  10.7 us
    all_to_all x1, starting transfers between devices, on_device(): lax.all_to_all(exposure, PA, split_axis=0, concat_axis=3, tiled=True)  7.14 us
    all_gather x1, waiting for transfers between devices, whole_of(): nearer = lax.all_gather(value, axes[-1], axis=dim, tiled=True)  4.55 us
  transfers between devices with their start and end apart: 4, of which 4 were waited for; matrix products, arithmetic and copies ran while one was open for 3% of the time, Pallas kernels for 0%

commit v1 on v0

v1 whole, which is shorter than its diff:
```python
import functools

import jax
import jax.numpy as jnp
from jax import lax
from jax.experimental import pallas as pl
from jax.experimental.pallas import tpu as pltpu
from jax.sharding import PartitionSpec as P

BF = jnp.bfloat16
F32 = jnp.float32
K = 64
SETS = 32
DATES = 16
LANES = 128
ROWS = 80
GROUPS = 32
STEPS = 8
PIECE = 128
PIECES = 2
NZ, NX, NPA, NSA = 8, 4, 32, 8
LOG2E = 1.4426950408889634
LN2 = 0.6931471805599453
MESH = pl.DeviceIdType.MESH


def ring(delta, extent):
    return min(delta, extent - delta)


OFFSETS = sorted(
    ((dz, dx) for dz in range(NZ) for dx in range(NX)),
    key=lambda o: (ring(o[0], NZ) + ring(o[1], NX), ring(o[0], NZ), o[0] > NZ // 2, o[1]),
)


def shifted(me, offset):
    z, x = me // NX, lax.rem(me, NX)
    return lax.rem(z + offset[0], NZ) * NX + lax.rem(x + offset[1], NX)


def back(offset):
    return ((NZ - offset[0]) % NZ, (NX - offset[1]) % NX)


def parts_of(value):
    high = value.astype(BF).astype(F32)
    rest = value - high
    middle = rest.astype(BF).astype(F32)
    return high, middle, rest - middle


def kernel(
    blocks, pick, factors, weights, terms, scale, shift, discount, set_pd, own_pd,
    profile_out, xva_out, total_out,
    tiles, shocked, flat, sides, staged, members_ref, coef_row, coefs, sums, outbox, inbox, near_out, near_in,
    send_sems, tile_sems, out_sems, in_sems, near_send, near_recv,
):
    pa = lax.axis_index("pa")
    sa = lax.axis_index("sa")

    barrier = pltpu.get_barrier_semaphore()
    for offset in OFFSETS[1:]:
        pl.semaphore_signal(barrier, inc=1, device_id={"pa": shifted(pa, offset)}, device_id_type=MESH)
    for hop in range(1, NSA):
        pl.semaphore_signal(barrier, inc=1, device_id={"sa": lax.rem(sa + hop, NSA)}, device_id_type=MESH)

    coef_row[...] = jnp.zeros_like(coef_row)
    coef_row[0:1, 0:16] = set_pd[...]
    coef_row[0:1, 16:32] = set_pd[...]
    coef_row[0:1, 32:48] = own_pd[...]
    coef_row[0:1, 48:64] = own_pd[...]
    coef = coef_row[0:1, :]
    ends = []
    running = jnp.int32(0)
    for m in range(SETS):
        running = running + blocks[m]
        ends.append(running)
    row = lax.broadcasted_iota(jnp.int32, (16, LANES), 0)
    for half in range(2):
        block = 2 * pa + half
        owner = jnp.int32(0)
        for end in ends:
            owner = owner + jnp.where(end <= block, 1, 0).astype(jnp.int32)
        lanes = slice(half * LANES, (half + 1) * LANES)
        notional = terms[0:1, lanes].astype(F32)
        strike = parts_of(terms[1:2, lanes].astype(F32) * LOG2E)
        rows = [*strike, notional, jnp.full((1, LANES), owner.astype(F32))]
        if half == 0:
            rows.extend(parts_of(coef))
        block_rows = jnp.zeros((16, LANES), F32)
        for i, value in enumerate(rows):
            block_rows = jnp.where(row == i, value, block_rows)
        tiles[0, half, 0:K] = weights[:, lanes]
        tiles[0, half, K:ROWS] = block_rows.astype(BF)

    for k in range(K):
        flat[k * DATES:(k + 1) * DATES, :] = factors[k].astype(F32)
    ones = jnp.where(lax.broadcasted_iota(jnp.int32, (K, LANES), 0) < 3, 1.0, 0.0).astype(BF)
    none = jnp.zeros((K, LANES), BF)
    for s in range(2):
        which = pick[s]
        scales = jnp.broadcast_to(scale[pl.ds(which, 1), :], (LANES, K)).T
        shifts = jnp.broadcast_to(shift[pl.ds(which, 1), :], (LANES, K)).T
        for d in range(DATES):
            g = s * DATES + d
            base = flat[pl.ds(d, K, stride=DATES), :]
            value = (scales * base + shifts).astype(BF).astype(F32) * LOG2E
            high = value.astype(BF)
            shocked[g, 0:K] = high
            shocked[g, K:2 * K] = ones
            shocked[g, 2 * K:3 * K] = (value - high.astype(F32)).astype(BF)
            shocked[g, 3 * K:4 * K] = none

    pl.semaphore_wait(barrier, NPA - 1 + NSA - 1)

    def tile_copy(k, target):
        return pltpu.make_async_remote_copy(
            src_ref=tiles.at[0], dst_ref=tiles.at[k], send_sem=send_sems.at[k], recv_sem=tile_sems.at[k],
            device_id={"pa": target}, device_id_type=MESH,
        )

    for k in range(1, NPA):
        tile_copy(k, shifted(pa, back(OFFSETS[k]))).start()

    def members(s):
        halves = []
        for half in range(2):
            info = tiles[s, half, K:ROWS].astype(F32)
            ids = lax.broadcasted_iota(jnp.int32, (SETS, LANES), 0).astype(F32)
            halves.append(jnp.where(ids == info[4:5, :], info[3:4, :], 0.0).astype(BF))
        return jnp.concatenate(halves, 1)

    def prepare(s, slot):
        for half in range(2):
            tile = jnp.concatenate([tiles[s, half], jnp.zeros((LANES - ROWS, LANES), BF)], 0)
            sides[slot, half * LANES:(half + 1) * LANES] = tile.T

    def softplus2(x):
        y = lax.log2(1.0 + lax.exp2(jnp.minimum(x, 100.0)))
        return jnp.maximum(y, x).astype(BF)

    def body(levels, nets):
        def push_shocked(q, j):
            g = (2 * (j % STEPS) + q) * 2
            both = jnp.concatenate([shocked[g], shocked[g + 1]], 1)
            pltpu.matmul_push_rhs(both, staging_register=0, mxu_index=q)

        def level(q, j, p, slot):
            side = sides[slot, p * PIECE:(p + 1) * PIECE]
            pltpu.matmul_acc_lhs(
                levels[q][j % 2][p], jnp.concatenate([side, side], 1), load_staged_rhs=0 if p == 0 else None
            )

        def net(q, j, chosen):
            values = staged[q, j % 2]
            pltpu.matmul_push_rhs(jnp.concatenate([values[0], values[1]], 1), staging_register=1, mxu_index=q)
            pltpu.matmul_acc_lhs(nets[q][j], chosen, load_staged_rhs=1)

        for q in range(2):
            for acc in nets[q]:
                pltpu.matmul_pop(acc)
            for r in range(2):
                for p in range(PIECES):
                    pltpu.matmul_pop(levels[q][r][p])
        prepare(0, 0)
        for j in range(2):
            for q in range(2):
                push_shocked(q, j)
                for p in range(PIECES):
                    level(q, j, p, 0)
        members_ref[...] = jnp.zeros_like(members_ref)
        staged[...] = jnp.zeros_like(staged)

        def shard(s, carry):
            @pl.when(s < NPA - 1)
            def _():
                tile_copy(s + 1, pa).wait_recv()

            chosen = members(s)
            prepare(lax.min(s + 1, NPA - 1), (s + 1) % 2)
            for j in range(STEPS):
                slot = (s + (j + 2) // STEPS) % 2
                for q in range(2):
                    push_shocked(q, j + 2)
                for p in range(PIECES):
                    for q in range(2):
                        x = pltpu.matmul_pop(levels[q][j % 2][p])
                        level(q, j + 2, p, slot)
                        value = softplus2(x)
                        for h in range(2):
                            staged[q, j % 2, h, p * PIECE:(p + 1) * PIECE] = value[:, h * LANES:(h + 1) * LANES]
                for q in range(2):
                    net(q, (j - 1) % STEPS, chosen if j else members_ref[...])
            members_ref[...] = chosen
            return carry

        lax.fori_loop(0, NPA, shard, 0)
        for q in range(2):
            net(q, STEPS - 1, members_ref[...])
            for r in range(2):
                for p in range(PIECES):
                    pltpu.matmul_pop(levels[q][r][p])

        lane = lax.broadcasted_iota(jnp.int32, (SETS, LANES), 1)
        partial = jnp.zeros((SETS, LANES), F32)
        for j in range(STEPS):
            for q in range(2):
                netted = pltpu.matmul_pop(nets[q][j])
                for h in range(2):
                    g = (2 * j + q) * 2 + h
                    d = g % DATES
                    exposure = netted[:, h * LANES:(h + 1) * LANES] * (0.0625 * LN2) * discount[d:d + 1, :].astype(F32)
                    positive = jnp.sum(jnp.maximum(exposure, 0.0), axis=1, keepdims=True)
                    negative = jnp.sum(jnp.minimum(exposure, 0.0), axis=1, keepdims=True)
                    partial = jnp.where(lane == g, positive, partial)
                    partial = jnp.where(lane == GROUPS + g, negative, partial)
        sums[...] = partial

    acc = lambda q, m: pltpu.ACC(q)((m, 256), F32)
    pl.run_scoped(
        body,
        [[[acc(q, PIECE) for _ in range(PIECES)] for _ in range(2)] for q in range(2)],
        [[acc(q, SETS) for _ in range(STEPS)] for q in range(2)],
    )

    for k in range(NPA):
        info = tiles[k, 0, K:ROWS].astype(F32)
        coefs[pl.ds(shifted(pa, OFFSETS[k]), 1), :] = info[5:6, :] + info[6:7, :] + info[7:8, :]
    partial = sums[...] * (1.0 / (NPA * LANES))
    totals = jnp.sum(partial * coefs[...], axis=0, keepdims=True)
    rows = partial + pltpu.roll(jnp.broadcast_to(totals, (8, LANES)), 64, 1)[0:1, :]
    for n in range(SETS):
        outbox[n] = rows[n:n + 1, :]

    def row_copy(k, target):
        return pltpu.make_async_remote_copy(
            src_ref=outbox.at[target], dst_ref=inbox.at[k], send_sem=out_sems.at[k], recv_sem=in_sems.at[k],
            device_id={"pa": target}, device_id_type=MESH,
        )

    for k in range(NPA - 1, 0, -1):
        row_copy(k, shifted(pa, OFFSETS[k])).start()
    inbox[0] = outbox[pa]
    for k in range(1, NPA):
        row_copy(k, shifted(pa, OFFSETS[k])).wait_recv()
    mine = jnp.sum(inbox[...], axis=0)

    lane = lax.broadcasted_iota(jnp.int32, (1, LANES), 1)
    weighted = mine * coef
    first = lax.rem(lane // DATES, 2) == 0
    upper = lane >= 64

    def lane_sum(value, mask):
        return jnp.sum(jnp.where(mask, value, 0.0), axis=1, keepdims=True)

    adjust = [lane_sum(weighted, first), lane_sum(weighted, jnp.logical_not(first))]
    total = [
        lane_sum(mine, jnp.logical_and(first, upper)),
        lane_sum(mine, jnp.logical_and(jnp.logical_not(first), upper)),
    ]
    near_out[...] = jnp.broadcast_to(adjust[0] + adjust[1], (1, LANES))

    def near_copy(hop, target):
        return pltpu.make_async_remote_copy(
            src_ref=near_out, dst_ref=near_in.at[hop], send_sem=near_send.at[hop], recv_sem=near_recv.at[hop],
            device_id={"sa": target}, device_id_type=MESH,
        )

    for hop in range(1, NSA):
        near_copy(hop, lax.rem(sa + hop, NSA)).start()
    near_in[0] = near_out[...]

    columns = jnp.broadcast_to(mine, (8, LANES)).T
    pair = lax.broadcasted_iota(jnp.int32, (DATES, 2), 1) == 0
    for sign in range(2):
        low = columns[sign * 32:sign * 32 + 16, 0:2]
        high = columns[sign * 32 + 16:sign * 32 + 32, 0:2]
        profile_out[sign] = jnp.where(pair, low, high)
    two = lax.broadcasted_iota(jnp.int32, (1, 2), 1) == 0
    total_out[...] = jnp.where(two, total[0], total[1])

    for hop in range(1, NSA):
        near_copy(hop, lax.rem(sa + hop, NSA)).wait_recv()
    mean = jnp.sum(near_in[...], axis=0)[:, 0:1] / (2 * NSA)
    xva_out[...] = jnp.where(two, adjust[0] - mean, adjust[1] - mean)

    for k in range(1, NPA):
        tile_copy(k, pa).wait_send()
        row_copy(k, shifted(pa, OFFSETS[k])).wait_send()
    for hop in range(1, NSA):
        near_copy(hop, sa).wait_send()


def on_device(
    factors, trade_weights, payoff_terms, set_blocks, shock_pick, shock_scale, shock_shift, discount, set_pd, own_pd
):
    vmem = pl.BlockSpec(memory_space=pltpu.VMEM)
    smem = pl.BlockSpec(memory_space=pltpu.SMEM)
    profile, xva, total = pl.pallas_call(
        kernel,
        out_shape=(
            jax.ShapeDtypeStruct((2, DATES, 2), F32),
            jax.ShapeDtypeStruct((1, 2), F32),
            jax.ShapeDtypeStruct((1, 2), F32),
        ),
        in_specs=[smem, smem] + [vmem] * 8,
        out_specs=(vmem, vmem, vmem),
        scratch_shapes=[
            pltpu.VMEM((NPA, 2, ROWS, LANES), BF),
            pltpu.VMEM((GROUPS, 256, LANES), BF),
            pltpu.VMEM((K * DATES, LANES), F32),
            pltpu.VMEM((2, 256, LANES), BF),
            pltpu.VMEM((2, 2, 2, 256, LANES), BF),
            pltpu.VMEM((SETS, 256), BF),
            pltpu.VMEM((8, LANES), F32),
            pltpu.VMEM((SETS, LANES), F32),
            pltpu.VMEM((SETS, LANES), F32),
            pltpu.VMEM((SETS, 1, LANES), F32),
            pltpu.VMEM((NPA, 1, LANES), F32),
            pltpu.VMEM((1, LANES), F32),
            pltpu.VMEM((NSA, 1, LANES), F32),
            pltpu.SemaphoreType.DMA((NPA,)),
            pltpu.SemaphoreType.DMA((NPA,)),
            pltpu.SemaphoreType.DMA((NPA,)),
            pltpu.SemaphoreType.DMA((NPA,)),
            pltpu.SemaphoreType.DMA((NSA,)),
            pltpu.SemaphoreType.DMA((NSA,)),
        ],
        compiler_params=pltpu.CompilerParams(
            collective_id=0, has_side_effects=True, vmem_limit_bytes=24 << 20
        ),
        name="valuation",
    )(
        set_blocks, shock_pick, factors, trade_weights, payoff_terms, shock_scale, shock_shift, discount, set_pd,
        own_pd.reshape(1, DATES),
    )
    return profile.reshape(2, 1, DATES, 2), xva, total.reshape(2)


def solution(mesh):
    return jax.shard_map(
        on_device,
        mesh=mesh,
        in_specs=(
            P(None, None, "pa"), P(None, "pa"), P(None, "pa"), P(), P("sa"), P(), P(), P(None, "pa"),
            P("pa", None), P(),
        ),
        out_specs=(P(None, "pa", None, "sa"), P("pa", "sa"), P("sa")),
        check_vma=False,
    )
```

time: 225 us -> 79.5 us (0.35)
  matrix products: 99.2 us -> 0 us
  Pallas kernels: 0 us -> 70.3 us
  blocking collectives: 41.4 us -> 0 us
  waiting for transfers between devices: 28 us -> 0 us
  starting transfers between devices: 22.7 us -> 0 us
  between operations: 14.8 us -> 0.67 us
  other arithmetic: 11 us -> 0 us
    dot_general x10 -> x0, matrix products: 99.2 us -> none  [the longest x8 97.4 us: net_trades(): return jnp.dot(members, values, preferred_element_type=jnp.float32)]
    pallas_call x0 -> x1, Pallas kernels: none -> 70.3 us  [on_device(): pl.pallas_call(kernel, out_shape=(jax.ShapeDtypeStruct((2, DATES, 2), F32...]
    all_gather x3 -> x0, blocking collectives: 41.4 us -> none  [whole_of(): nearer = lax.all_gather(value, axes[-1], axis=dim, tiled=True)]
    all_to_all x3 -> x0, waiting for transfers between devices: 23.5 us -> none  [the longest x1 12.8 us: on_device(): lax.all_to_all(exposure, PA, split_axis=0, concat_axis=3, tiled=True)]
    all_to_all x3 -> x0, starting transfers between devices: 22.7 us -> none  [the longest x2 15.6 us: from_everyone(): return lax.all_to_all(copies, axis, split_axis=0, concat_axis=0, tiled=True)]
    unnamed x14 -> x22, local copies, waits for them, and re-layouts: 0.38 us -> 7.49 us
    convert_element_type x19 -> x0, other arithmetic: 6.22 us -> none  [the longest x8 4.46 us: on_device(): shocked = (scale_rows[:, None, :, None] * factors.astype(jnp.float32)[:,...]
    all_gather x1 -> x0, waiting for transfers between devices: 4.55 us -> none  [whole_of(): nearer = lax.all_gather(value, axes[-1], axis=dim, tiled=True)]
  transfers between devices with their start and end apart: 4 -> 0, of which waited for: 4 -> 0; matrix products, arithmetic and copies ran while one was open for 3% -> 0% of each run, Pallas kernels for 0% -> 0%
where the time goes in v1:
time: 79.5 us; the launch traced here: 79.1 us
  Pallas kernels  70.3 us (88%)
  local copies, waits for them, and re-layouts  8.15 us (10%)
    pallas_call x1, Pallas kernels, on_device(): pl.pallas_call(kernel, out_shape=(jax.ShapeDtypeStruct((2, DATES, 2), F32...  70.3 us
    unnamed x22, local copies, waits for them, and re-layouts  7.49 us

profile of v1, /device:TPU:1, one launch (start us, length us, event | category | flops | bytes accessed | tf_op | source)
XLA Modules:
  0.0 79.1 jit_solution(4256078875492648535)
XLA Ops:
  0.6 0.0 copy-start.6
  0.6 0.0 copy-start.5
  0.7 0.6 copy-done.6
  1.3 0.0 copy-done.5
  1.3 0.0 copy-start
  1.3 0.9 %copy-done = bf16[64,16,128]{2,1,0:T(8,128)(2,1)S(1)} copy-done((bf16[64,16,128]{2,1,0:T(8,128)(2,1)S(1)}, bf16[64,16,128]{2,1,0:T(8,128)(2,1)}, u32[]{:S(2)}) %copy-start) | copy-done | bytes 262168
  2.3 0.0 copy-start.1
  2.3 0.8 copy-done.1
  3.0 0.0 copy-start.2
  3.0 0.7 copy-done.2
  3.8 0.0 copy-start.3
  3.8 0.7 copy-done.3
  4.5 0.0 copy-start.4
  4.5 0.7 copy-done.4
  5.2 0.0 copy-start.7
  5.2 0.7 copy-done.7
  5.8 0.0 copy-start.8
  5.8 0.7 copy-done.8
  6.5 0.0 copy-start.9
  6.5 0.7 copy-done.9
  7.1 70.3 %valuation.1 = (f32[2,16,2]{2,1,0:T(8,128)S(1)}, f32[1,2]{1,0:T(1,128)S(1)}, f32[1,2]{1,0:T(1,128)S(1)}) custom-call(s32[32]{0:T(128)S(1)} %copy-done.6, s32[2]{0:T(128)S(1)} %copy-done.7, bf16[64,16,128]{2,1,0:T(8,128)(2,1)S(1)} %copy-done, bf16[64,256]{1,0:T(8,128)(2,1)S(1)} %copy-done.1, bf16[2,256]{1,0:T(2,128)(2,1)S(1)} %copy-done.5, ...), custom_call_target="tpu_custom_call" | custom-call | tf_op jit(solution)/shard_map/valuation/pallas_call | solution.py:300
  77.4 0.7 copy.13
  78.1 0.5 copy.16
  78.6 0.5 copy.17
Async XLA Ops:
  0.6 0.7 copy-start.6
  0.6 0.7 copy-start.5
  1.3 0.9 %copy-start = (bf16[64,16,128]{2,1,0:T(8,128)(2,1)S(1)}, bf16[64,16,128]{2,1,0:T(8,128)(2,1)}, u32[]{:S(2)}) copy-start(bf16[64,16,128]{2,1,0:T(8,128)(2,1)} %factors.1) | copy-start | bytes 786436
  2.3 0.8 copy-start.1
  3.0 0.7 copy-start.2
  3.8 0.7 copy-start.3
  4.5 0.7 copy-start.4
  5.2 0.7 copy-start.7
  5.8 0.7 copy-start.8
  6.5 0.7 copy-start.9

commit v2 on v1

--- a/solution.py
+++ b/solution.py
@@ -51,19 +51,33 @@
 
 
 def kernel(
-    blocks, pick, factors, weights, terms, scale, shift, discount, set_pd, own_pd,
-    profile_out, xva_out, total_out,
-    tiles, shocked, flat, sides, staged, members_ref, coef_row, coefs, sums, outbox, inbox, near_out, near_in,
-    send_sems, tile_sems, out_sems, in_sems, near_send, near_recv,
+    *refs,
 ):
+    hbm, refs = refs[:10], refs[10:]
+    result, refs = refs[0], refs[1:]
+    local, refs = refs[:10], refs[10:]
+    blocks, pick, factors, weights, terms, scale, shift, discount, set_pd, own_pd = local
+    (
+        tiles, shocked, flat, side0, side1, stage00, stage01, stage10, stage11, members_ref, coef_row, coefs, sums,
+        outbox, inbox, near_out, near_in,
+        load_sems, send_sems, tile_sems, out_sems, in_sems, near_send, near_recv,
+    ) = refs
+    sides = [side0, side1]
+    staged = [[stage00, stage01], [stage10, stage11]]
     pa = lax.axis_index("pa")
     sa = lax.axis_index("sa")
+    loads = [pltpu.make_async_copy(hbm[i], local[i], load_sems.at[i]) for i in range(10)]
+    for load in loads:
+        load.start()
 
     barrier = pltpu.get_barrier_semaphore()
     for offset in OFFSETS[1:]:
         pl.semaphore_signal(barrier, inc=1, device_id={"pa": shifted(pa, offset)}, device_id_type=MESH)
     for hop in range(1, NSA):
         pl.semaphore_signal(barrier, inc=1, device_id={"sa": lax.rem(sa + hop, NSA)}, device_id_type=MESH)
+
+    for load in loads:
+        load.wait()
 
     coef_row[...] = jnp.zeros_like(coef_row)
     coef_row[0:1, 0:16] = set_pd[...]
@@ -134,7 +148,7 @@
     def prepare(s, slot):
         for half in range(2):
             tile = jnp.concatenate([tiles[s, half], jnp.zeros((LANES - ROWS, LANES), BF)], 0)
-            sides[slot, half * LANES:(half + 1) * LANES] = tile.T
+            sides[slot][half * LANES:(half + 1) * LANES] = tile.T
 
     def softplus2(x):
         y = lax.log2(1.0 + lax.exp2(jnp.minimum(x, 100.0)))
@@ -147,13 +161,13 @@
             pltpu.matmul_push_rhs(both, staging_register=0, mxu_index=q)
 
         def level(q, j, p, slot):
-            side = sides[slot, p * PIECE:(p + 1) * PIECE]
+            side = sides[slot][p * PIECE:(p + 1) * PIECE]
             pltpu.matmul_acc_lhs(
                 levels[q][j % 2][p], jnp.concatenate([side, side], 1), load_staged_rhs=0 if p == 0 else None
             )
 
         def net(q, j, chosen):
-            values = staged[q, j % 2]
+            values = staged[q][j % 2]
             pltpu.matmul_push_rhs(jnp.concatenate([values[0], values[1]], 1), staging_register=1, mxu_index=q)
             pltpu.matmul_acc_lhs(nets[q][j], chosen, load_staged_rhs=1)
 
@@ -170,17 +184,14 @@
                 for p in range(PIECES):
                     level(q, j, p, 0)
         members_ref[...] = jnp.zeros_like(members_ref)
-        staged[...] = jnp.zeros_like(staged)
-
-        def shard(s, carry):
-            @pl.when(s < NPA - 1)
-            def _():
-                tile_copy(s + 1, pa).wait_recv()
-
-            chosen = members(s)
-            prepare(lax.min(s + 1, NPA - 1), (s + 1) % 2)
+        for q in range(2):
+            staged[q][1][...] = jnp.zeros_like(stage00)
+
+        def shard(s, parity, chosen, before):
             for j in range(STEPS):
-                slot = (s + (j + 2) // STEPS) % 2
+                if j == 0:
+                    prepare(lax.min(s + 1, NPA - 1), 1 - parity)
+                slot = parity if j + 2 < STEPS else 1 - parity
                 for q in range(2):
                     push_shocked(q, j + 2)
                 for p in range(PIECES):
@@ -189,13 +200,26 @@
                         level(q, j + 2, p, slot)
                         value = softplus2(x)
                         for h in range(2):
-                            staged[q, j % 2, h, p * PIECE:(p + 1) * PIECE] = value[:, h * LANES:(h + 1) * LANES]
+                            staged[q][j % 2][h, p * PIECE:(p + 1) * PIECE] = value[:, h * LANES:(h + 1) * LANES]
                 for q in range(2):
-                    net(q, (j - 1) % STEPS, chosen if j else members_ref[...])
-            members_ref[...] = chosen
+                    net(q, (j - 1) % STEPS, chosen if j else before)
+
+        def pair_of_shards(i, carry):
+            tile_copy(2 * i + 1, pa).wait_recv()
+
+            @pl.when(i < NPA // 2 - 1)
+            def _():
+                tile_copy(2 * i + 2, pa).wait_recv()
+
+            before = members_ref[...]
+            for parity in range(2):
+                chosen = members(2 * i + parity)
+                shard(2 * i + parity, parity, chosen, before)
+                before = chosen
+            members_ref[...] = before
             return carry
 
-        lax.fori_loop(0, NPA, shard, 0)
+        lax.fori_loop(0, NPA // 2, pair_of_shards, 0)
         for q in range(2):
             net(q, STEPS - 1, members_ref[...])
             for r in range(2):
@@ -271,19 +295,13 @@
         near_copy(hop, lax.rem(sa + hop, NSA)).start()
     near_in[0] = near_out[...]
 
-    columns = jnp.broadcast_to(mine, (8, LANES)).T
-    pair = lax.broadcasted_iota(jnp.int32, (DATES, 2), 1) == 0
-    for sign in range(2):
-        low = columns[sign * 32:sign * 32 + 16, 0:2]
-        high = columns[sign * 32 + 16:sign * 32 + 32, 0:2]
-        profile_out[sign] = jnp.where(pair, low, high)
-    two = lax.broadcasted_iota(jnp.int32, (1, 2), 1) == 0
-    total_out[...] = jnp.where(two, total[0], total[1])
-
     for hop in range(1, NSA):
         near_copy(hop, lax.rem(sa + hop, NSA)).wait_recv()
     mean = jnp.sum(near_in[...], axis=0)[:, 0:1] / (2 * NSA)
-    xva_out[...] = jnp.where(two, adjust[0] - mean, adjust[1] - mean)
+    row = mine
+    for i, value in enumerate([adjust[0] - mean, adjust[1] - mean, *total]):
+        row = jnp.where(lane == 64 + i, value, row)
+    result[...] = row
 
     for k in range(1, NPA):
         tile_copy(k, pa).wait_send()
@@ -292,26 +310,37 @@
         near_copy(hop, sa).wait_send()
 
 
+def spread(row, profile_out, xva_out, total_out):
+    values = row[...]
+    for sign in range(2):
+        for s in range(2):
+            start = sign * 32 + s * 16
+            profile_out[sign, s:s + 1, :] = values[:, start:start + DATES]
+    xva_out[...] = values[:, 64:66]
+    total_out[...] = values[:, 66:68]
+
+
 def on_device(
     factors, trade_weights, payoff_terms, set_blocks, shock_pick, shock_scale, shock_shift, discount, set_pd, own_pd
 ):
     vmem = pl.BlockSpec(memory_space=pltpu.VMEM)
-    smem = pl.BlockSpec(memory_space=pltpu.SMEM)
-    profile, xva, total = pl.pallas_call(
+    arrays = [
+        set_blocks, shock_pick, factors, trade_weights, payoff_terms, shock_scale, shock_shift, discount, set_pd,
+        own_pd.reshape(1, DATES),
+    ]
+    row = pl.pallas_call(
         kernel,
-        out_shape=(
-            jax.ShapeDtypeStruct((2, DATES, 2), F32),
-            jax.ShapeDtypeStruct((1, 2), F32),
-            jax.ShapeDtypeStruct((1, 2), F32),
-        ),
-        in_specs=[smem, smem] + [vmem] * 8,
-        out_specs=(vmem, vmem, vmem),
+        out_shape=jax.ShapeDtypeStruct((1, LANES), F32),
+        in_specs=[pl.BlockSpec(memory_space=pl.ANY)] * 10,
+        out_specs=vmem,
         scratch_shapes=[
+            *(pltpu.SMEM(a.shape, a.dtype) for a in arrays[:2]),
+            *(pltpu.VMEM(a.shape, a.dtype) for a in arrays[2:]),
             pltpu.VMEM((NPA, 2, ROWS, LANES), BF),
             pltpu.VMEM((GROUPS, 256, LANES), BF),
             pltpu.VMEM((K * DATES, LANES), F32),
-            pltpu.VMEM((2, 256, LANES), BF),
-            pltpu.VMEM((2, 2, 2, 256, LANES), BF),
+            *(pltpu.VMEM((256, LANES), BF) for _ in range(2)),
+            *(pltpu.VMEM((2, 256, LANES), BF) for _ in range(4)),
             pltpu.VMEM((SETS, 256), BF),
             pltpu.VMEM((8, LANES), F32),
             pltpu.VMEM((SETS, LANES), F32),
@@ -320,6 +349,7 @@
             pltpu.VMEM((NPA, 1, LANES), F32),
             pltpu.VMEM((1, LANES), F32),
             pltpu.VMEM((NSA, 1, LANES), F32),
+            pltpu.SemaphoreType.DMA((10,)),
             pltpu.SemaphoreType.DMA((NPA,)),
             pltpu.SemaphoreType.DMA((NPA,)),
             pltpu.SemaphoreType.DMA((NPA,)),
@@ -328,14 +358,22 @@
             pltpu.SemaphoreType.DMA((NSA,)),
         ],
         compiler_params=pltpu.CompilerParams(
-            collective_id=0, has_side_effects=True, vmem_limit_bytes=24 << 20
+            collective_id=0, has_side_effects=True, vmem_limit_bytes=60 << 20
         ),
         name="valuation",
-    )(
-        set_blocks, shock_pick, factors, trade_weights, payoff_terms, shock_scale, shock_shift, discount, set_pd,
-        own_pd.reshape(1, DATES),
-    )
-    return profile.reshape(2, 1, DATES, 2), xva, total.reshape(2)
+    )(*arrays)
+    profile, xva, total = pl.pallas_call(
+        spread,
+        out_shape=(
+            jax.ShapeDtypeStruct((2, 2, DATES), F32),
+            jax.ShapeDtypeStruct((1, 2), F32),
+            jax.ShapeDtypeStruct((1, 2), F32),
+        ),
+        in_specs=[vmem],
+        out_specs=(vmem, vmem, vmem),
+        name="spread",
+    )(row)
+    return profile.transpose(0, 2, 1).reshape(2, 1, DATES, 2), xva, total.reshape(2)
 
 
 def solution(mesh):

time: 79.5 us -> 70.9 us (0.89)
  local copies, waits for them, and re-layouts: 8.15 us -> 0 us
    unnamed x22 -> x0, local copies, waits for them, and re-layouts: 7.49 us -> none
    pallas_call x1 -> x2, Pallas kernels: 70.3 us -> 70.1 us  [the longest x1 68.9 us: on_device(): pl.pallas_call(kernel, out_shape=jax.ShapeDtypeStruct((1, LANES), F32), i...]
where the time goes in v2:
time: 70.9 us; the launch traced here: 70.8 us
  Pallas kernels  70.1 us (99%)
    pallas_call x1, Pallas kernels, on_device(): pl.pallas_call(kernel, out_shape=jax.ShapeDtypeStruct((1, LANES), F32), i...  68.9 us

profile of v2, /device:TPU:1, one launch (start us, length us, event | category | flops | bytes accessed | tf_op | source)
XLA Modules:
  0.0 70.8 jit_solution(13133600283491312602)
XLA Ops:
  0.6 68.9 %valuation.1.row = f32[1,128]{1,0:T(1,128)} custom-call(s32[32]{0:T(128)} %refs_0_.1, s32[2]{0:T(128)} %refs_1_.1, bf16[64,16,128]{2,1,0:T(8,128)(2,1)} %refs_2_.1, bf16[64,256]{1,0:T(8,128)(2,1)} %refs_3_.1, bf16[2,256]{1,0:T(2,128)(2,1)} %refs_4_.1, f32[32,64]{1,0:T(8,128)} %refs_5_.1, f32[32,64]{1,0:T(8,128)} %refs_6_.1, bf16[16,128]{1,0:T(8,128)(2,1)} %refs_7_.1, ...), custom_call_target="tpu_custom_call" | custom-call | tf_op jit(solution)/shard_map/valuation/pallas_call | solution.py:331
  69.5 1.3 %spread.1 = (f32[2,2,16]{2,1,0:T(2,128)}, f32[1,2]{1,0:T(1,128)}, f32[1,2]{1,0:T(1,128)}) custom-call(f32[1,128]{1,0:T(1,128)} %valuation.1.row), custom_call_target="tpu_custom_call" | custom-call | tf_op jit(solution)/shard_map/spread/pallas_call | solution.py:365

commit v3 on v2

--- a/solution.py
+++ b/solution.py
@@ -22,6 +22,8 @@
 LOG2E = 1.4426950408889634
 LN2 = 0.6931471805599453
 MESH = pl.DeviceIdType.MESH
+FIRST, LAST, AHEAD = 4, 14, 2
+BOTH = range(1, 2 * FIRST + 1)
 
 
 def ring(delta, extent):
@@ -60,8 +62,9 @@
     (
         tiles, shocked, flat, side0, side1, stage00, stage01, stage10, stage11, members_ref, coef_row, coefs, sums,
         outbox, inbox, near_out, near_in,
-        load_sems, send_sems, tile_sems, out_sems, in_sems, near_send, near_recv,
+        load_sems, send_sems, tile_sems, relay_sems, out_sems, in_sems, near_send, near_recv,
     ) = refs
+    core = lax.rem(lax.axis_index("sa"), 2)
     sides = [side0, side1]
     staged = [[stage00, stage01], [stage10, stage11]]
     pa = lax.axis_index("pa")
@@ -76,8 +79,8 @@
     for hop in range(1, NSA):
         pl.semaphore_signal(barrier, inc=1, device_id={"sa": lax.rem(sa + hop, NSA)}, device_id_type=MESH)
 
-    for load in loads:
-        load.wait()
+    for i in (0, 3, 4, 8, 9):
+        loads[i].wait()
 
     coef_row[...] = jnp.zeros_like(coef_row)
     coef_row[0:1, 0:16] = set_pd[...]
@@ -108,6 +111,8 @@
         tiles[0, half, 0:K] = weights[:, lanes]
         tiles[0, half, K:ROWS] = block_rows.astype(BF)
 
+    for i in (1, 2, 5, 6, 7):
+        loads[i].wait()
     for k in range(K):
         flat[k * DATES:(k + 1) * DATES, :] = factors[k].astype(F32)
     ones = jnp.where(lax.broadcasted_iota(jnp.int32, (K, LANES), 0) < 3, 1.0, 0.0).astype(BF)
@@ -134,8 +139,21 @@
             device_id={"pa": target}, device_id_type=MESH,
         )
 
-    for k in range(1, NPA):
+    def relay(k):
+        return pltpu.make_async_remote_copy(
+            src_ref=tiles.at[k], dst_ref=tiles.at[k], send_sem=relay_sems.at[k], recv_sem=tile_sems.at[k],
+            device_id={"sa": sa + 1 - 2 * core}, device_id_type=MESH,
+        )
+
+    def half_of(k):
+        targets = [shifted(pa, back(OFFSETS[k + c])) for c in range(2)]
+        return tile_copy(k + core, jnp.where(core == 0, targets[0], targets[1]))
+
+    for k in BOTH:
         tile_copy(k, shifted(pa, back(OFFSETS[k]))).start()
+    for i in range(FIRST, LAST + 1):
+        half_of(2 * i + 1).start()
+    tile_copy(NPA - 1, shifted(pa, back(OFFSETS[NPA - 1]))).start()
 
     def members(s):
         halves = []
@@ -205,11 +223,24 @@
                     net(q, (j - 1) % STEPS, chosen if j else before)
 
         def pair_of_shards(i, carry):
-            tile_copy(2 * i + 1, pa).wait_recv()
-
-            @pl.when(i < NPA // 2 - 1)
+            @pl.when(i < FIRST)
             def _():
+                tile_copy(2 * i + 1, pa).wait_recv()
                 tile_copy(2 * i + 2, pa).wait_recv()
+
+            @pl.when(jnp.logical_and(i >= FIRST - AHEAD, i <= LAST - AHEAD))
+            def _():
+                k = 2 * (i + AHEAD) + 1 + core
+                tile_copy(k, pa).wait_recv()
+                relay(k).start()
+
+            @pl.when(jnp.logical_and(i >= FIRST, i <= LAST))
+            def _():
+                tile_copy(2 * i + 2 - core, pa).wait_recv()
+
+            @pl.when(i > LAST)
+            def _():
+                tile_copy(NPA - 1, pa).wait_recv()
 
             before = members_ref[...]
             for parity in range(2):
@@ -303,8 +334,12 @@
         row = jnp.where(lane == 64 + i, value, row)
     result[...] = row
 
+    for k in (*BOTH, NPA - 1):
+        tile_copy(k, pa).wait_send()
+    for i in range(FIRST, LAST + 1):
+        half_of(2 * i + 1).wait_send()
+        relay(2 * i + 1 + core).wait_send()
     for k in range(1, NPA):
-        tile_copy(k, pa).wait_send()
         row_copy(k, shifted(pa, OFFSETS[k])).wait_send()
     for hop in range(1, NSA):
         near_copy(hop, sa).wait_send()
@@ -354,6 +389,7 @@
             pltpu.SemaphoreType.DMA((NPA,)),
             pltpu.SemaphoreType.DMA((NPA,)),
             pltpu.SemaphoreType.DMA((NPA,)),
+            pltpu.SemaphoreType.DMA((NPA,)),
             pltpu.SemaphoreType.DMA((NSA,)),
             pltpu.SemaphoreType.DMA((NSA,)),
         ],

time: 70.9 us -> 72.9 us (1.028)
  Pallas kernels: 70.1 us -> 72.1 us
    pallas_call x1, Pallas kernels: 68.9 us -> 70.8 us  [on_device(): pl.pallas_call(kernel, out_shape=jax.ShapeDtypeStruct((1, LANES), F32), i...]
where the time goes in v3:
time: 72.9 us; the launch traced here: 72.7 us
  Pallas kernels  72.1 us (99%)
    pallas_call x1, Pallas kernels, on_device(): pl.pallas_call(kernel, out_shape=jax.ShapeDtypeStruct((1, LANES), F32), i...  70.8 us

profile of v3, /device:TPU:1, one launch (start us, length us, event | category | flops | bytes accessed | tf_op | source)
XLA Modules:
  0.0 72.7 jit_solution(90631918720723215)
XLA Ops:
  0.6 70.8 %valuation.1.row = f32[1,128]{1,0:T(1,128)} custom-call(s32[32]{0:T(128)} %refs_0_.1, s32[2]{0:T(128)} %refs_1_.1, bf16[64,16,128]{2,1,0:T(8,128)(2,1)} %refs_2_.1, bf16[64,256]{1,0:T(8,128)(2,1)} %refs_3_.1, bf16[2,256]{1,0:T(2,128)(2,1)} %refs_4_.1, f32[32,64]{1,0:T(8,128)} %refs_5_.1, f32[32,64]{1,0:T(8,128)} %refs_6_.1, bf16[16,128]{1,0:T(8,128)(2,1)} %refs_7_.1, ...), custom_call_target="tpu_custom_call" | custom-call | tf_op jit(solution)/shard_map/valuation/pallas_call | solution.py:366
  71.5 1.3 %spread.1 = (f32[2,2,16]{2,1,0:T(2,128)}, f32[1,2]{1,0:T(1,128)}, f32[1,2]{1,0:T(1,128)}) custom-call(f32[1,128]{1,0:T(1,128)} %valuation.1.row), custom_call_target="tpu_custom_call" | custom-call | tf_op jit(solution)/shard_map/spread/pallas_call | solution.py:401

commit v4 on v2

--- a/solution.py
+++ b/solution.py
@@ -24,14 +24,8 @@
 MESH = pl.DeviceIdType.MESH
 
 
-def ring(delta, extent):
-    return min(delta, extent - delta)
-
-
-OFFSETS = sorted(
-    ((dz, dx) for dz in range(NZ) for dx in range(NX)),
-    key=lambda o: (ring(o[0], NZ) + ring(o[1], NX), ring(o[0], NZ), o[0] > NZ // 2, o[1]),
-)
+OFFSETS = [(dz, dx) for dz in (0, 1, 7, 2, 6, 3, 5, 4) for dx in (0, 1, 3, 2)]
+NEAR = (1, 2, 3, 4, 8)
 
 
 def shifted(me, offset):
@@ -71,13 +65,13 @@
         load.start()
 
     barrier = pltpu.get_barrier_semaphore()
-    for offset in OFFSETS[1:]:
-        pl.semaphore_signal(barrier, inc=1, device_id={"pa": shifted(pa, offset)}, device_id_type=MESH)
+    for k in NEAR:
+        pl.semaphore_signal(barrier, inc=1, device_id={"pa": shifted(pa, OFFSETS[k])}, device_id_type=MESH)
     for hop in range(1, NSA):
         pl.semaphore_signal(barrier, inc=1, device_id={"sa": lax.rem(sa + hop, NSA)}, device_id_type=MESH)
 
-    for load in loads:
-        load.wait()
+    for i in (0, 3, 4, 8, 9):
+        loads[i].wait()
 
     coef_row[...] = jnp.zeros_like(coef_row)
     coef_row[0:1, 0:16] = set_pd[...]
@@ -108,6 +102,8 @@
         tiles[0, half, 0:K] = weights[:, lanes]
         tiles[0, half, K:ROWS] = block_rows.astype(BF)
 
+    for i in (1, 2, 5, 6, 7):
+        loads[i].wait()
     for k in range(K):
         flat[k * DATES:(k + 1) * DATES, :] = factors[k].astype(F32)
     ones = jnp.where(lax.broadcasted_iota(jnp.int32, (K, LANES), 0) < 3, 1.0, 0.0).astype(BF)
@@ -126,16 +122,24 @@
             shocked[g, 2 * K:3 * K] = (value - high.astype(F32)).astype(BF)
             shocked[g, 3 * K:4 * K] = none
 
-    pl.semaphore_wait(barrier, NPA - 1 + NSA - 1)
-
-    def tile_copy(k, target):
+    pl.semaphore_wait(barrier, len(NEAR) + NSA - 1)
+
+    def tile_copy(source, k, target):
         return pltpu.make_async_remote_copy(
-            src_ref=tiles.at[0], dst_ref=tiles.at[k], send_sem=send_sems.at[k], recv_sem=tile_sems.at[k],
+            src_ref=tiles.at[source], dst_ref=tiles.at[k], send_sem=send_sems.at[k], recv_sem=tile_sems.at[k],
             device_id={"pa": target}, device_id_type=MESH,
         )
 
-    for k in range(1, NPA):
-        tile_copy(k, shifted(pa, back(OFFSETS[k]))).start()
+    def arrived(k):
+        tile_copy(k, k, pa).wait_recv()
+
+    def pass_on(source, k):
+        odd = lax.rem(k // NX, 2)
+        target = lax.rem(pa // NX + 1 + (NZ - 2) * odd, NZ) * NX + lax.rem(pa, NX)
+        tile_copy(source, k, target).start()
+
+    for k in NEAR:
+        tile_copy(0, k, shifted(pa, back(OFFSETS[k]))).start()
 
     def members(s):
         halves = []
@@ -183,48 +187,65 @@
                 push_shocked(q, j)
                 for p in range(PIECES):
                     level(q, j, p, 0)
-        members_ref[...] = jnp.zeros_like(members_ref)
-        for q in range(2):
-            staged[q][1][...] = jnp.zeros_like(stage00)
-
-        def shard(s, parity, chosen, before):
+
+        def shard(s, parity, chosen, before, first=False, last=False):
             for j in range(STEPS):
-                if j == 0:
-                    prepare(lax.min(s + 1, NPA - 1), 1 - parity)
+                if first and j == 4:
+                    arrived(1)
+                    pass_on(1, 5)
+                    pass_on(1, 9)
+                if not last and j == (4 if first else 0):
+                    prepare(s + 1, 1 - parity)
                 slot = parity if j + 2 < STEPS else 1 - parity
-                for q in range(2):
-                    push_shocked(q, j + 2)
+                ahead = not last or j + 2 < STEPS
+                if ahead:
+                    for q in range(2):
+                        push_shocked(q, j + 2)
                 for p in range(PIECES):
                     for q in range(2):
                         x = pltpu.matmul_pop(levels[q][j % 2][p])
-                        level(q, j + 2, p, slot)
+                        if ahead:
+                            level(q, j + 2, p, slot)
                         value = softplus2(x)
                         for h in range(2):
                             staged[q][j % 2][h, p * PIECE:(p + 1) * PIECE] = value[:, h * LANES:(h + 1) * LANES]
-                for q in range(2):
-                    net(q, (j - 1) % STEPS, chosen if j else before)
+                if j or not first:
+                    for q in range(2):
+                        net(q, (j - 1) % STEPS, chosen if j else before)
+
+        chosen = members(0)
+        shard(0, 0, chosen, None, first=True)
+        members_ref[...] = chosen
 
         def pair_of_shards(i, carry):
-            tile_copy(2 * i + 1, pa).wait_recv()
-
-            @pl.when(i < NPA // 2 - 1)
+            arrived(2 * i + 2)
+            arrived(2 * i + 3)
+
+            @pl.when(i == 0)
             def _():
-                tile_copy(2 * i + 2, pa).wait_recv()
+                for k in (2, 3):
+                    pass_on(k, k + 4)
+                    pass_on(k, k + 8)
+
+            @pl.when(jnp.logical_and(i >= 1, i <= 10))
+            def _():
+                for k in (2 * i + 2, 2 * i + 3):
+                    pass_on(k, k + 8)
 
             before = members_ref[...]
-            for parity in range(2):
-                chosen = members(2 * i + parity)
-                shard(2 * i + parity, parity, chosen, before)
+            for parity in (1, 0):
+                s = 2 * i + 2 - parity
+                chosen = members(s)
+                shard(s, parity, chosen, before)
                 before = chosen
             members_ref[...] = before
             return carry
 
-        lax.fori_loop(0, NPA // 2, pair_of_shards, 0)
+        lax.fori_loop(0, NPA // 2 - 1, pair_of_shards, 0)
+        chosen = members(NPA - 1)
+        shard(NPA - 1, 1, chosen, members_ref[...], last=True)
         for q in range(2):
-            net(q, STEPS - 1, members_ref[...])
-            for r in range(2):
-                for p in range(PIECES):
-                    pltpu.matmul_pop(levels[q][r][p])
+            net(q, STEPS - 1, chosen)
 
         lane = lax.broadcasted_iota(jnp.int32, (SETS, LANES), 1)
         partial = jnp.zeros((SETS, LANES), F32)
@@ -304,7 +325,7 @@
     result[...] = row
 
     for k in range(1, NPA):
-        tile_copy(k, pa).wait_send()
+        tile_copy(0, k, pa).wait_send()
         row_copy(k, shifted(pa, OFFSETS[k])).wait_send()
     for hop in range(1, NSA):
         near_copy(hop, sa).wait_send()

time: 70.9 us -> 67.9 us (0.958)
  Pallas kernels: 70.1 us -> 67.1 us
    pallas_call x1, Pallas kernels: 68.9 us -> 65.9 us  [on_device(): pl.pallas_call(kernel, out_shape=jax.ShapeDtypeStruct((1, LANES), F32), i...]
where the time goes in v4:
time: 67.9 us; the launch traced here: 67.8 us
  Pallas kernels  67.1 us (99%)
    pallas_call x1, Pallas kernels, on_device(): pl.pallas_call(kernel, out_shape=jax.ShapeDtypeStruct((1, LANES), F32), i...  65.9 us

profile of v4, /device:TPU:1, one launch (start us, length us, event | category | flops | bytes accessed | tf_op | source)
XLA Modules:
  0.0 67.8 jit_solution(15144217550376103700)
XLA Ops:
  0.6 65.9 %valuation.1.row = f32[1,128]{1,0:T(1,128)} custom-call(s32[32]{0:T(128)} %refs_0_.1, s32[2]{0:T(128)} %refs_1_.1, bf16[64,16,128]{2,1,0:T(8,128)(2,1)} %refs_2_.1, bf16[64,256]{1,0:T(8,128)(2,1)} %refs_3_.1, bf16[2,256]{1,0:T(2,128)(2,1)} %refs_4_.1, f32[32,64]{1,0:T(8,128)} %refs_5_.1, f32[32,64]{1,0:T(8,128)} %refs_6_.1, bf16[16,128]{1,0:T(8,128)(2,1)} %refs_7_.1, ...), custom_call_target="tpu_custom_call" | custom-call | tf_op jit(solution)/shard_map/valuation/pallas_call | solution.py:352
  66.5 1.3 %spread.1 = (f32[2,2,16]{2,1,0:T(2,128)}, f32[1,2]{1,0:T(1,128)}, f32[1,2]{1,0:T(1,128)}) custom-call(f32[1,128]{1,0:T(1,128)} %valuation.1.row), custom_call_target="tpu_custom_call" | custom-call | tf_op jit(solution)/shard_map/spread/pallas_call | solution.py:386
